TPU v7x, 32 devices: a whole 2x2x4 slice. The times are simulated.
32 devices in a mesh: leaf: 8 (over y, x, core), wide: 4 (over z).
Axes of the slice: x: 2, y: 2, z: 4, core: 2. Of those that a mesh axis runs over, the one named last changes fastest.
Arguments:
- source: bfloat16 [4, 8, 4, 256, 1024], P(None, 'leaf', 'wide'), may hold values from -6 to 6
- row_factors: bfloat16 [4, 4, 8, 4, 256, 512], P(None, None, 'leaf', 'wide'), may hold values from -0.25 to 0.25
- column_factors: bfloat16 [4, 4, 8, 4, 256, 512], P(None, None, 'leaf', 'wide'), may hold values from -0.25 to 0.25
Outputs:
- result: bfloat16 [4, 8, 4, 256, 1024], P(None, 'leaf', 'wide')
All inputs are finite; a program needn't handle non-finite values.
Results may differ from a plain program's by a relative error of at most 0.015.
Values may be sent and summed in bfloat16 or wider, within the bound.
A program may use at most 64 MiB of HBM per device.

v0:
```python
import jax
import jax.numpy as jnp
from jax import lax
from jax.sharding import PartitionSpec as P


def from_partner(value, axis, apart):
    mask = 2**apart
    pairs = [(source, source ^ mask) for source in range(lax.axis_size(axis))]
    return lax.ppermute(value, axis, pairs)


def combine(own_block, partner, is_lower, factors):
    rank_size = own_block.shape[1]
    leading = jnp.where(is_lower, own_block, partner)
    trailing = jnp.where(is_lower, partner, own_block)
    result = jnp.einsum(
        "brk,bkh->brh", factors[:, :, :rank_size], leading, preferred_element_type=jnp.float32
    )
    result = result + jnp.einsum(
        "brk,bkh->brh", factors[:, :, rank_size:], trailing, preferred_element_type=jnp.float32
    )
    return result.astype(jnp.bfloat16)


def row_cross(coeffs, factors, level_no):
    partner = from_partner(coeffs, "leaf", level_no)
    is_lower = lax.axis_index("leaf") >> level_no & 1 == 0
    return combine(coeffs, partner, is_lower, factors)


def column_cross(coeffs, factors, level_no):
    partner = from_partner(coeffs, "wide", level_no)
    is_lower = lax.axis_index("wide") >> level_no & 1 == 0
    return combine(coeffs, partner, is_lower, factors)


def local_level(coeffs, factors, stride):
    blocks, rank_size, rhs_count = coeffs.shape
    grouped = coeffs.reshape(blocks // (2 * stride), 2, stride, rank_size, rhs_count)
    partner = grouped[:, ::-1].reshape(blocks, rank_size, rhs_count)
    block_index = jnp.arange(blocks)
    is_lower = (block_index // stride % 2 == 0)[:, None, None]
    return combine(coeffs, partner, is_lower, factors)


def run_pass(coeffs, factors, axis_count, level_order, crosser):
    for level_no in level_order:
        stride_now = 1 << level_no
        if stride_now < axis_count:
            half_count = coeffs.shape[0] // 2
            first_part = crosser(coeffs[:half_count], factors[level_no, :half_count], level_no)
            second_part = crosser(coeffs[half_count:], factors[level_no, half_count:], level_no)
            coeffs = jnp.concatenate([first_part, second_part], axis=0)
        else:
            coeffs = local_level(coeffs, factors[level_no], stride_now // axis_count)
    return coeffs


def per_device(source, row_factors, column_factors):
    blocks = source.shape[0]
    rank_size = source.shape[3]
    rhs_count = source.shape[4]
    levels = row_factors.shape[0]
    coeffs = source.reshape(blocks, rank_size, rhs_count)
    forward = row_factors.reshape(levels, blocks, rank_size, 2 * rank_size)
    adjoint = column_factors.reshape(levels, blocks, rank_size, 2 * rank_size)
    coeffs = run_pass(coeffs, forward, lax.axis_size("leaf"), list(range(levels)), row_cross)
    coeffs = run_pass(
        coeffs, adjoint, lax.axis_size("wide"), list(reversed(range(levels))), column_cross
    )
    return coeffs.reshape(source.shape)


def solution(mesh):
    return jax.shard_map(
        per_device,
        mesh=mesh,
        in_specs=(
            P(None, "leaf", "wide", None, None),
            P(None, None, "leaf", "wide", None, None),
            P(None, None, "leaf", "wide", None, None),
        ),
        out_specs=P(None, "leaf", "wide", None, None),
        check_vma=False,
    )
```

profile of v0, /device:TPU:4, one launch (start us, length us, event | category | flops | bytes accessed | tf_op | source)
XLA Modules:
  0.0 246.2 jit_solution(1393760456822758358)
XLA Ops:
  0.0 2.5 slice_bitcast_fusion.3
  2.5 1.0 slice_bitcast_fusion.4
  4.0 3.1 %slice_bitcast_fusion.12 = (bf16[2,256,512]{2,1,0:T(8,128)(2,1)}, bf16[2,256,512]{2,1,0:T(8,128)(2,1)}, bf16[2,256,512]{2,1,0:T(8,128)(2,1)S(1)}, bf16[2,256,512...) fusion(bf16[4,4,256,512]{3,2,1,0:T(8,128)(2,1)} %bitcast.104), kind=kLoop, calls=%fused_computation.103 | loop fusion | bytes 6291456 | tf_op jit(solution)/shard_map/squeeze | solution.py:52
  7.1 1.8 fusion.38
  9.6 1.6 collective-permute-start.1
  12.9 2.3 slice_bitcast_fusion.2
  15.2 20.4 %collective-permute-done.1 = bf16[2,256,1024]{1,2,0:T(8,128)(2,1)S(1)} collective-permute-done((bf16[2,256,1024]{1,2,0:T(8,128)(2,1)S(1)}, bf16[2,256,1024]{1,2,0:T(8,128)(2,1)S(1)}, u32[]{:S(2)}, u32[]{:S(2)}) %collective-permute-start.1) | collective-permute-done | bytes 1048608 | tf_op jit(solution)/shard_map/ppermute | solution.py:10
  36.7 20.5 %collective-permute-done.4 = bf16[2,256,1024]{1,2,0:T(8,128)(2,1)S(1)} collective-permute-done((bf16[2,256,1024]{1,2,0:T(8,128)(2,1)S(1)}, bf16[2,256,1024]{1,2,0:T(8,128)(2,1)S(1)}, u32[]{:S(2)}, u32[]{:S(2)}) %collective-permute-start.4) | collective-permute-done | bytes 1048608 | tf_op jit(solution)/shard_map/ppermute | solution.py:10
  58.4 3.0 %slice_bitcast_fusion = (bf16[4,256,512]{2,1,0:T(8,128)(2,1)}, bf16[4,256,512]{2,1,0:T(8,128)(2,1)}) fusion(bf16[4,4,1,1,256,512]{5,4,1,3,2,0:T(8,128)(2,1)} %bitcast.106), kind=kLoop, calls=%fused_computation.32 | loop fusion | bytes 4194304 | tf_op jit(solution)/shard_map/squeeze | solution.py:56
  62.9 1.8 fusion.3
  64.7 17.8 %collective-permute-done.5 = bf16[2,256,1024]{1,2,0:T(8,128)(2,1)} collective-permute-done((bf16[2,256,1024]{1,2,0:T(8,128)(2,1)S(1)}, bf16[2,256,1024]{1,2,0:T(8,128)(2,1)}, u32[]{:S(2)}, u32[]{:S(2)}) %collective-permute-start.5) | collective-permute-done | bytes 1048608 | tf_op jit(solution)/shard_map/ppermute | solution.py:10
  83.0 1.7 fusion.6
  84.7 1.5 pad_maximum_fusion
  86.2 3.1 %rev.9 = bf16[2,2,1,256,1024]{3,4,1,0,2:T(8,128)(2,1)} reverse(bf16[2,2,1,256,1024]{3,4,1,0,2:T(8,128)(2,1)} %bitcast.103), dimensions={1} | reverse | bytes 4194304 | tf_op jit(solution)/shard_map/rev | solution.py:41
  89.3 2.0 bitcast_select_fusion.4
  92.9 1.5 rev.10
  94.3 2.0 bitcast_select_fusion.2
  97.9 1.5 rev.11
  99.4 2.0 bitcast_select_fusion
  102.2 1.0 fusion
  103.2 1.5 fusion.97
  104.7 2.6 %collective-permute-start.6 = (bf16[2,256,1024]{1,2,0:T(8,128)(2,1)}, bf16[2,256,1024]{1,2,0:T(8,128)(2,1)S(1)}, u32[]{:S(2)}, u32[]{:S(2)}) collective-permute-start(bf16[2,256,1024]{1,2,0:T(8,128)(2,1)} %get-tuple-element.23), channel_id=1, source_target_pairs={{0,2},{1,3},{2,0},{3,1},{4,6},{5,7},{6,4},{7,5},{8,10},{9,11},{10,... | collective-permute-start | bytes 3145736 | tf_op jit(solution)/shard_map/ppermute | solution.py:10
  107.6 2.7 %slice_bitcast_fusion.7 = (bf16[2,256,512]{2,1,0:T(8,128)(2,1)}, bf16[2,256,512]{2,1,0:T(8,128)(2,1)}, bf16[2,256,512]{2,1,0:T(8,128)(2,1)S(1)}, bf16[2,256,512]{2,1,0:T(8,128)(2,1)S(1)}) fusion(bf16[4,4,256,512]{3,2,1,0:T(8,128)(2,1)} %bitcast.107), kind=kLoop, calls=%fused_computation.89 | loop fusion | bytes 4194304 | tf_op jit(solution)/shard_map/squeeze | solution.py:52
  110.3 64.9 %collective-permute-done.6 = bf16[2,256,1024]{1,2,0:T(8,128)(2,1)S(1)} collective-permute-done((bf16[2,256,1024]{1,2,0:T(8,128)(2,1)}, bf16[2,256,1024]{1,2,0:T(8,128)(2,1)S(1)}, u32[]{:S(2)}, u32[]{:S(2)}) %collective-permute-start.6) | collective-permute-done | bytes 1048608 | tf_op jit(solution)/shard_map/ppermute | solution.py:10
  177.2 19.5 %collective-permute-done.8 = bf16[2,256,1024]{1,2,0:T(8,128)(2,1)} collective-permute-done((bf16[2,256,1024]{1,2,0:T(8,128)(2,1)}, bf16[2,256,1024]{1,2,0:T(8,128)(2,1)}, u32[]{:S(2)}, u32[]{:S(2)}) %collective-permute-start.8) | collective-permute-done | bytes 1048608 | tf_op jit(solution)/shard_map/ppermute | solution.py:10
  196.7 1.7 fusion.14
  198.4 1.5 fusion.9
  200.5 18.7 %collective-permute-done.7 = bf16[2,256,1024]{1,2,0:T(8,128)(2,1)} collective-permute-done((bf16[2,256,1024]{1,2,0:T(8,128)(2,1)S(1)}, bf16[2,256,1024]{1,2,0:T(8,128)(2,1)}, u32[]{:S(2)}, u32[]{:S(2)}) %collective-permute-start.7) | collective-permute-done | bytes 1048608 | tf_op jit(solution)/shard_map/ppermute | solution.py:10
  219.2 1.8 fusion.17
  221.5 19.9 %collective-permute-done.9 = bf16[2,256,1024]{1,2,0:T(8,128)(2,1)S(1)} collective-permute-done((bf16[2,256,1024]{1,2,0:T(8,128)(2,1)}, bf16[2,256,1024]{1,2,0:T(8,128)(2,1)S(1)}, u32[]{:S(2)}, u32[]{:S(2)}) %collective-permute-start.9) | collective-permute-done | bytes 1048608 | tf_op jit(solution)/shard_map/ppermute | solution.py:10
  241.9 1.7 fusion.10
  243.9 2.4 copy.12
  (52 shorter events, 15.0 us)
Async XLA Ops:
  0.0 2.5 %copy-start = (bf16[4,1,1,256,1024]{4,3,2,1,0:T(8,128)(2,1)S(1)}, bf16[4,1,1,256,1024]{4,3,2,1,0:T(8,128)(2,1)}, u32[]{:S(2)}) copy-start(bf16[4,1,1,256,1024]{4,3,2,1,0:T(8,128)(2,1)} %param.3) | copy-start | bytes 6291460
  2.5 4.7 %collective-permute-start = (bf16[2,256,1024]{2,1,0:T(8,128)(2,1)}, bf16[2,256,1024]{2,1,0:T(8,128)(2,1)}, u32[]{:S(2)}, u32[]{:S(2)}) collective-permute-start(bf16[2,256,1024]{2,1,0:T(8,128)(2,1)} %slice_bitcast_fusion.3), channel_id=1, source_target_pairs={{0,4},{4,0},{8,12},{12,8},{16,20},{20,16},{24,28},{28,24},{1,5},{5... | collective-permute-start | bytes 3145736 | tf_op jit(solution)/shard_map/ppermute | solution.py:10
  3.5 7.6 %collective-permute-start.3 = (bf16[2,256,1024]{2,1,0:T(8,128)(2,1)}, bf16[2,256,1024]{2,1,0:T(8,128)(2,1)S(1)}, u32[]{:S(2)}, u32[]{:S(2)}) collective-permute-start(bf16[2,256,1024]{2,1,0:T(8,128)(2,1)} %slice_bitcast_fusion.4), channel_id=1, source_target_pairs={{0,4},{4,0},{8,12},{12,8},{16,20},{20,16},{24,28},{28,24},{1,5},{5... | collective-permute-start | bytes 3145736 | tf_op jit(solution)/shard_map/ppermute | solution.py:10
  9.6 26.1 %collective-permute-start.1 = (bf16[2,256,1024]{1,2,0:T(8,128)(2,1)S(1)}, bf16[2,256,1024]{1,2,0:T(8,128)(2,1)S(1)}, u32[]{:S(2)}, u32[]{:S(2)}) collective-permute-start(bf16[2,256,1024]{1,2,0:T(8,128)(2,1)S(1)} %fusion.1), channel_id=1, source_target_pairs={{0,8},{4,12},{8,0},{12,4},{16,24},{20,28},{24,16},{28,20},{1,9},{5... | collective-permute-start | bytes 3145736 | tf_op jit(solution)/shard_map/ppermute | solution.py:10
  12.3 44.8 %collective-permute-start.4 = (bf16[2,256,1024]{1,2,0:T(8,128)(2,1)S(1)}, bf16[2,256,1024]{1,2,0:T(8,128)(2,1)S(1)}, u32[]{:S(2)}, u32[]{:S(2)}) collective-permute-start(bf16[2,256,1024]{1,2,0:T(8,128)(2,1)S(1)} %fusion.4), channel_id=1, source_target_pairs={{0,8},{4,12},{8,0},{12,4},{16,24},{20,28},{24,16},{28,20},{1,9},{5... | collective-permute-start | bytes 3145736 | tf_op jit(solution)/shard_map/ppermute | solution.py:10
  36.6 24.9 %collective-permute-start.2 = (bf16[2,256,1024]{1,2,0:T(8,128)(2,1)S(1)}, bf16[2,256,1024]{1,2,0:T(8,128)(2,1)S(1)}, u32[]{:S(2)}, u32[]{:S(2)}) collective-permute-start(bf16[2,256,1024]{1,2,0:T(8,128)(2,1)S(1)} %fusion.2), channel_id=1, source_target_pairs={{0,16},{4,20},{8,24},{12,28},{16,0},{20,4},{24,8},{28,12},{1,17},{... | collective-permute-start | bytes 3145736 | tf_op jit(solution)/shard_map/ppermute | solution.py:10
  58.1 24.4 %collective-permute-start.5 = (bf16[2,256,1024]{1,2,0:T(8,128)(2,1)S(1)}, bf16[2,256,1024]{1,2,0:T(8,128)(2,1)}, u32[]{:S(2)}, u32[]{:S(2)}) collective-permute-start(bf16[2,256,1024]{1,2,0:T(8,128)(2,1)S(1)} %fusion.5), channel_id=1, source_target_pairs={{0,16},{4,20},{8,24},{12,28},{16,0},{20,4},{24,8},{28,12},{1,17},{... | collective-permute-start | bytes 3145736 | tf_op jit(solution)/shard_map/ppermute | solution.py:10
  58.4 4.0 %copy-start.7 = (bf16[2,256,512]{2,1,0:T(8,128)(2,1)S(1)}, bf16[2,256,512]{2,1,0:T(8,128)(2,1)}, u32[]{:S(2)}) copy-start(bf16[2,256,512]{2,1,0:T(8,128)(2,1)} %get-tuple-element.17) | copy-start | bytes 1572868
  61.5 1.0 copy-start.1
  62.9 19.6 %copy-start.6 = (bf16[2,256,512]{2,1,0:T(8,128)(2,1)S(1)}, bf16[2,256,512]{2,1,0:T(8,128)(2,1)}, u32[]{:S(2)}) copy-start(bf16[2,256,512]{2,1,0:T(8,128)(2,1)} %get-tuple-element.18) | copy-start | bytes 1572868
  89.3 2.0 copy-start.3
  94.3 2.0 copy-start.5
  99.4 2.0 copy-start.4
  104.7 70.5 %collective-permute-start.6 = (bf16[2,256,1024]{1,2,0:T(8,128)(2,1)}, bf16[2,256,1024]{1,2,0:T(8,128)(2,1)S(1)}, u32[]{:S(2)}, u32[]{:S(2)}) collective-permute-start(bf16[2,256,1024]{1,2,0:T(8,128)(2,1)} %get-tuple-element.23), channel_id=1, source_target_pairs={{0,2},{1,3},{2,0},{3,1},{4,6},{5,7},{6,4},{7,5},{8,10},{9,11},{10,... | collective-permute-start | bytes 3145736 | tf_op jit(solution)/shard_map/ppermute | solution.py:10
  107.3 89.5 %collective-permute-start.8 = (bf16[2,256,1024]{1,2,0:T(8,128)(2,1)}, bf16[2,256,1024]{1,2,0:T(8,128)(2,1)}, u32[]{:S(2)}, u32[]{:S(2)}) collective-permute-start(bf16[2,256,1024]{1,2,0:T(8,128)(2,1)} %get-tuple-element.24), channel_id=1, source_target_pairs={{0,2},{1,3},{2,0},{3,1},{4,6},{5,7},{6,4},{7,5},{8,10},{9,11},{10,... | collective-permute-start | bytes 3145736 | tf_op jit(solution)/shard_map/ppermute | solution.py:10
  175.2 1.0 copy-start.2
  177.1 42.1 %collective-permute-start.7 = (bf16[2,256,1024]{1,2,0:T(8,128)(2,1)S(1)}, bf16[2,256,1024]{1,2,0:T(8,128)(2,1)}, u32[]{:S(2)}, u32[]{:S(2)}) collective-permute-start(bf16[2,256,1024]{1,2,0:T(8,128)(2,1)S(1)} %fusion.7), channel_id=1, source_target_pairs={{0,1},{1,0},{2,3},{3,2},{4,5},{5,4},{6,7},{7,6},{8,9},{9,8},{10,11... | collective-permute-start | bytes 3145736 | tf_op jit(solution)/shard_map/ppermute | solution.py:10
  199.9 41.6 %collective-permute-start.9 = (bf16[2,256,1024]{1,2,0:T(8,128)(2,1)}, bf16[2,256,1024]{1,2,0:T(8,128)(2,1)S(1)}, u32[]{:S(2)}, u32[]{:S(2)}) collective-permute-start(bf16[2,256,1024]{1,2,0:T(8,128)(2,1)} %fusion.9), channel_id=1, source_target_pairs={{0,1},{1,0},{2,3},{3,2},{4,5},{5,4},{6,7},{7,6},{8,9},{9,8},{10,11... | collective-permute-start | bytes 3145736 | tf_op jit(solution)/shard_map/ppermute | solution.py:10
  219.2 1.8 copy-start.9
  221.0 20.5 %copy-start.8 = (bf16[2,256,512]{2,1,0:T(8,128)(2,1)S(1)}, bf16[2,256,512]{2,1,0:T(8,128)(2,1)}, u32[]{:S(2)}) copy-start(bf16[2,256,512]{2,1,0:T(8,128)(2,1)} %get-tuple-element.12) | copy-start | bytes 1572868
where the time goes:
time: 249 us; the launch traced here: 246 us
  waiting for transfers between devices  182 us (73%)
  local copies, waits for them, and re-layouts  26.5 us (11%)
  matrix products  23.3 us (9%)
  other arithmetic  7.77 us (3%)
  starting transfers between devices  6.69 us (3%)
    ppermute x10, waiting for transfers between devices, from_partner(): return lax.ppermute(value, axis, pairs)  182 us
    dot_general x13, matrix products, combine(): jnp.einsum('brk,bkh->brh', factors[:, :, :rank_size], leading, preferred_...  12.1 us
    dot_general x13, matrix products, combine(): jnp.einsum('brk,bkh->brh', factors[:, :, rank_size:], trailing, preferred...  11.2 us
    ppermute x10, starting transfers between devices, from_partner(): return lax.ppermute(value, axis, pairs)  6.69 us
    select_n x3, other arithmetic, combine(): trailing = jnp.where(is_lower, partner, own_block)  6.07 us
    rev x3, local copies, waits for them, and re-layouts, local_level(): partner = grouped[:, ::-1].reshape(blocks, rank_size, rhs_count)  6.01 us
    squeeze x2, local copies, waits for them, and re-layouts, run_pass(): factors[level_no, :half_count]  5.81 us
    squeeze x2, local copies, waits for them, and re-layouts, run_pass(): coeffs = local_level(coeffs, factors[level_no], stride_now // axis_count)  5.35 us
  transfers between devices with their start and end apart: 10, of which 7 were waited for; matrix products, arithmetic and copies ran while one was open for 11% of the time, Pallas kernels for 0%

commit v1 on v0

v1 whole, which is shorter than its diff:
```python
import functools

import jax
import jax.numpy as jnp
from jax import lax
from jax.experimental import pallas as pl
from jax.experimental.pallas import tpu as pltpu
from jax.sharding import PartitionSpec as P

MESH = pl.DeviceIdType.MESH
CHUNK = 128


def make_groups(levels, sizes):
    order = [("leaf", 0, n) for n in range(levels)]
    order += [("wide", 1, n) for n in reversed(range(levels))]
    groups, pending = [], []
    for axis, which, n in order:
        stride = 1 << n
        if stride < sizes[axis]:
            groups.append(dict(axis=axis, mask=stride, slot=which * levels + n, local=[]))
        elif groups:
            groups[-1]["local"].append((stride // sizes[axis], which * levels + n))
        else:
            pending.append(n)
    assert not pending
    return groups


def kernel(groups, levels, src, row, col, out, own0, held, obuf, rcv, fac, tmp,
           src_sem, fac_sem, send_sem, recv_sem, out_sem):
    blocks, rank, _ = src.shape
    chunks = rcv.shape[1]
    count = len(groups)
    me = {a: lax.axis_index(a) for a in ("leaf", "wide")}
    bits = [lax.rem(lax.div(me[g["axis"]], g["mask"]), 2) for g in groups]
    partner = [
        {g["axis"]: me[g["axis"]] + g["mask"] * (1 - 2 * bit)} for g, bit in zip(groups, bits)
    ]

    def src_copy(k):
        cols = pl.ds(pl.multiple_of(k * CHUNK, CHUNK), CHUNK)
        return pltpu.make_async_copy(src.at[:, :, cols], own0.at[k], src_sem.at[k])

    def src_send(k):
        cols = pl.ds(pl.multiple_of(k * CHUNK, CHUNK), CHUNK)
        return pltpu.make_async_remote_copy(
            src_ref=src.at[:, :, cols], dst_ref=rcv.at[0, k], send_sem=send_sem.at[0],
            recv_sem=recv_sem.at[0, k, 0], device_id=partner[0], device_id_type=MESH)

    def fac_copies(slot, bit):
        ref = (row if slot < levels else col).at[slot % levels]
        halves = []
        for j in range(2):
            at = j * rank if bit is None else (bit if j == 0 else 1 - bit) * rank
            if bit is not None:
                at = pl.multiple_of(at, rank)
            halves.append(pltpu.make_async_copy(
                ref.at[:, :, pl.ds(at, rank)], fac.at[slot, j], fac_sem.at[slot, j]))
        return halves

    def all_fac(g):
        copies = fac_copies(groups[g]["slot"], bits[g])
        for _, slot in groups[g]["local"]:
            copies += fac_copies(slot, None)
        return copies

    def send(g, k, b):
        return pltpu.make_async_remote_copy(
            src_ref=held.at[g - 1, k, b], dst_ref=rcv.at[g, k, b], send_sem=send_sem.at[g],
            recv_sem=recv_sem.at[g, k, b], device_id=partner[g], device_id_type=MESH)

    src_copy(0).start()
    for c in all_fac(0):
        c.start()

    barrier = pltpu.get_barrier_semaphore()
    for g in range(count):
        pl.semaphore_signal(barrier, inc=1, device_id=partner[g], device_id_type=MESH)
    pl.semaphore_wait(barrier, count)

    src_send(0).start()
    for k in range(1, chunks):
        src_copy(k).start()
        src_send(k).start()
    for g in range(1, count):
        for c in all_fac(g):
            c.start()

    def mul(slot, b, first, second):
        total = jnp.dot(fac[slot, 0, b], first, preferred_element_type=jnp.float32)
        total = total + jnp.dot(fac[slot, 1, b], second, preferred_element_type=jnp.float32)
        return total.astype(jnp.bfloat16)

    def step(g, k):
        group = groups[g]

        @pl.when(k == 0)
        def _():
            for c in all_fac(g):
                c.wait()

        if g == 0:
            src_copy(k).wait()
            src_send(k).wait_recv()

        def finish(b, value):
            if g + 1 < count:
                held[g, k, b] = value
                send(g + 1, k, b).start()
            else:
                obuf[k, b] = value
                cols = pl.ds(pl.multiple_of(k * CHUNK, CHUNK), CHUNK)
                pltpu.make_async_copy(
                    obuf.at[k, b], out.at[b, :, cols], out_sem).start()

        for b in range(blocks):
            if g:
                send(g, k, b).wait_recv()
            own = own0[k, b] if g == 0 else held[g - 1, k, b]
            value = mul(group["slot"], b, own, rcv[g, k, b])
            if group["local"]:
                tmp[0, b] = value
            else:
                finish(b, value)
        for n, (stride, slot) in enumerate(group["local"]):
            now = n % 2
            for b in range(blocks):
                low = b - stride * (b // stride % 2)
                value = mul(slot, b, tmp[now, low], tmp[now, low + stride])
                if n + 1 < len(group["local"]):
                    tmp[1 - now, b] = value
                else:
                    finish(b, value)

    cut = sum(g["axis"] == "leaf" for g in groups)
    order = [0] + list(reversed(range(1, cut))) + list(range(max(cut, 1), count))

    def body(t, _):
        for g in order:
            k = t - g

            @pl.when((k >= 0) & (k < chunks))
            def _():
                step(g, k)

        return 0

    lax.fori_loop(0, chunks + count - 1, body, 0)

    pltpu.make_async_copy(own0, own0, send_sem.at[0]).wait()
    for g in range(1, count):
        pltpu.make_async_copy(held.at[g - 1], held.at[g - 1], send_sem.at[g]).wait()
    pltpu.make_async_copy(obuf, obuf, out_sem).wait()


def per_device(sizes, source, row_factors, column_factors):
    blocks, rank, rhs = source.shape[0], source.shape[3], source.shape[4]
    levels = row_factors.shape[0]
    groups = make_groups(levels, sizes)
    count = len(groups)
    chunks = rhs // CHUNK
    bf = jnp.bfloat16
    part = (chunks, blocks, rank, CHUNK)
    result = pl.pallas_call(
        functools.partial(kernel, groups, levels),
        out_shape=jax.ShapeDtypeStruct((blocks, rank, rhs), bf),
        in_specs=[pl.BlockSpec(memory_space=pl.ANY)] * 3,
        out_specs=pl.BlockSpec(memory_space=pl.ANY),
        scratch_shapes=[
            pltpu.VMEM(part, bf),
            pltpu.VMEM((count - 1,) + part, bf),
            pltpu.VMEM(part, bf),
            pltpu.VMEM((count,) + part, bf),
            pltpu.VMEM((2 * levels, 2, blocks, rank, rank), bf),
            pltpu.VMEM((2, blocks, rank, CHUNK), bf),
            pltpu.SemaphoreType.DMA((chunks,)),
            pltpu.SemaphoreType.DMA((2 * levels, 2)),
            pltpu.SemaphoreType.DMA((count,)),
            pltpu.SemaphoreType.DMA((count, chunks, blocks)),
            pltpu.SemaphoreType.DMA,
        ],
        compiler_params=pltpu.CompilerParams(
            collective_id=0, has_side_effects=True, vmem_limit_bytes=60 * 2**20),
    )(
        source.reshape(blocks, rank, rhs),
        row_factors.reshape(levels, blocks, rank, 2 * rank),
        column_factors.reshape(levels, blocks, rank, 2 * rank),
    )
    return result.reshape(source.shape)


def solution(mesh):
    return jax.shard_map(
        functools.partial(per_device, dict(mesh.shape)),
        mesh=mesh,
        in_specs=(
            P(None, "leaf", "wide", None, None),
            P(None, None, "leaf", "wide", None, None),
            P(None, None, "leaf", "wide", None, None),
        ),
        out_specs=P(None, "leaf", "wide", None, None),
        check_vma=False,
    )
```

time: 249 us -> 123 us (0.49); the launches traced: 246 us -> 123 us
  waiting for transfers between devices: 182 us -> 0 us
  Pallas kernels: 0 us -> 120 us
  local copies, waits for them, and re-layouts: 26.5 us -> 3.08 us
  matrix products: 23.3 us -> 0 us
  other arithmetic: 7.77 us -> 0 us
  starting transfers between devices: 6.69 us -> 0 us
    ppermute x10 -> x0, waiting for transfers between devices: 182 us -> none  [from_partner(): return lax.ppermute(value, axis, pairs)]
    pallas_call x0 -> x1, Pallas kernels: none -> 120 us  [per_device(): pl.pallas_call(functools.partial(kernel, groups, levels), out_shape=jax.S...]
    dot_general x26 -> x0, matrix products: 23.3 us -> none  [the longest x13 12.1 us: combine(): jnp.einsum('brk,bkh->brh', factors[:, :, :rank_size], leading, preferred_...]
    squeeze x4 -> x0, local copies, waits for them, and re-layouts: 11.2 us -> none  [the longest x2 5.81 us: run_pass(): factors[level_no, :half_count]]
    ppermute x10 -> x0, starting transfers between devices: 6.69 us -> none  [from_partner(): return lax.ppermute(value, axis, pairs)]
    select_n x3 -> x0, other arithmetic: 6.07 us -> none  [combine(): trailing = jnp.where(is_lower, partner, own_block)]
    rev x3 -> x0, local copies, waits for them, and re-layouts: 6.01 us -> none  [local_level(): partner = grouped[:, ::-1].reshape(blocks, rank_size, rhs_count)]
    slice x3 -> x0, local copies, waits for them, and re-layouts: 5.01 us -> none  [the longest x2 3.97 us: run_pass(): coeffs[:half_count]]
  transfers between devices with their start and end apart: 10 -> 0, of which waited for: 7 -> 0; matrix products, arithmetic and copies ran while one was open for 11% -> 0% of each run, Pallas kernels for 0% -> 0%
where the time goes in v1:
time: 123 us
  Pallas kernels  120 us (98%)
  local copies, waits for them, and re-layouts  3.08 us (3%)
    pallas_call x1, Pallas kernels, per_device(): pl.pallas_call(functools.partial(kernel, groups, levels), out_shape=jax.S...  120 us
    unnamed x1, local copies, waits for them, and re-layouts  3.08 us

profile of v1, /device:TPU:4, one launch (start us, length us, event | category | flops | bytes accessed | tf_op | source)
XLA Modules:
  0.0 123.2 jit_solution(17240656323233290903)
XLA Ops:
  0.0 120.1 %shard_map.37 = bf16[4,256,1024]{2,1,0:T(8,128)(2,1)} custom-call(bf16[4,256,1024]{2,1,0:T(8,128)(2,1)} %bitcast.9, bf16[4,4,256,512]{3,2,1,0:T(8,128)(2,1)} %bitcast.7, bf16[4,4,256,512]{3,2,1,0:T(8,128)(2,1)} %bitcast.8), custom_call_target="tpu_custom_call" | custom-call | tf_op jit(solution)/shard_map/pallas_call | solution.py:165
  120.1 3.1 %copy.6 = bf16[4,1,1,256,1024]{4,3,2,1,0:T(8,128)(2,1)} copy(bf16[4,1,1,256,1024]{4,3,2,1,0:T(8,128)(2,1)} %bitcast.6) | data formatting | bytes 4194304

commit v2 on v1

--- a/solution.py
+++ b/solution.py
@@ -27,8 +27,8 @@
     return groups
 
 
-def kernel(groups, levels, src, row, col, out, own0, held, obuf, rcv, fac, tmp,
-           src_sem, fac_sem, send_sem, recv_sem, out_sem):
+def kernel(groups, levels, src, row, col, out, own0, held, rcv, fac, tmp,
+           src_sem, fac_sem, send_sem, recv_sem):
     blocks, rank, _ = src.shape
     chunks = rcv.shape[1]
     count = len(groups)
@@ -42,11 +42,11 @@
         cols = pl.ds(pl.multiple_of(k * CHUNK, CHUNK), CHUNK)
         return pltpu.make_async_copy(src.at[:, :, cols], own0.at[k], src_sem.at[k])
 
-    def src_send(k):
+    def src_send(k, b):
         cols = pl.ds(pl.multiple_of(k * CHUNK, CHUNK), CHUNK)
         return pltpu.make_async_remote_copy(
-            src_ref=src.at[:, :, cols], dst_ref=rcv.at[0, k], send_sem=send_sem.at[0],
-            recv_sem=recv_sem.at[0, k, 0], device_id=partner[0], device_id_type=MESH)
+            src_ref=src.at[b, :, cols], dst_ref=rcv.at[0, k, b], send_sem=send_sem.at[0],
+            recv_sem=recv_sem.at[0, k, b], device_id=partner[0], device_id_type=MESH)
 
     def fac_copies(slot, bit):
         ref = (row if slot < levels else col).at[slot % levels]
@@ -79,10 +79,12 @@
         pl.semaphore_signal(barrier, inc=1, device_id=partner[g], device_id_type=MESH)
     pl.semaphore_wait(barrier, count)
 
-    src_send(0).start()
+    for b in range(blocks):
+        src_send(0, b).start()
     for k in range(1, chunks):
         src_copy(k).start()
-        src_send(k).start()
+        for b in range(blocks):
+            src_send(k, b).start()
     for g in range(1, count):
         for c in all_fac(g):
             c.start()
@@ -102,21 +104,17 @@
 
         if g == 0:
             src_copy(k).wait()
-            src_send(k).wait_recv()
 
         def finish(b, value):
             if g + 1 < count:
                 held[g, k, b] = value
                 send(g + 1, k, b).start()
             else:
-                obuf[k, b] = value
                 cols = pl.ds(pl.multiple_of(k * CHUNK, CHUNK), CHUNK)
-                pltpu.make_async_copy(
-                    obuf.at[k, b], out.at[b, :, cols], out_sem).start()
+                out[b, :, cols] = value
 
         for b in range(blocks):
-            if g:
-                send(g, k, b).wait_recv()
+            (send(g, k, b) if g else src_send(k, b)).wait_recv()
             own = own0[k, b] if g == 0 else held[g - 1, k, b]
             value = mul(group["slot"], b, own, rcv[g, k, b])
             if group["local"]:
@@ -151,7 +149,6 @@
     pltpu.make_async_copy(own0, own0, send_sem.at[0]).wait()
     for g in range(1, count):
         pltpu.make_async_copy(held.at[g - 1], held.at[g - 1], send_sem.at[g]).wait()
-    pltpu.make_async_copy(obuf, obuf, out_sem).wait()
 
 
 def per_device(sizes, source, row_factors, column_factors):
@@ -164,13 +161,12 @@
     part = (chunks, blocks, rank, CHUNK)
     result = pl.pallas_call(
         functools.partial(kernel, groups, levels),
-        out_shape=jax.ShapeDtypeStruct((blocks, rank, rhs), bf),
+        out_shape=pltpu.VMEM((blocks, rank, rhs), bf),
         in_specs=[pl.BlockSpec(memory_space=pl.ANY)] * 3,
-        out_specs=pl.BlockSpec(memory_space=pl.ANY),
+        out_specs=pl.BlockSpec(memory_space=pltpu.VMEM),
         scratch_shapes=[
             pltpu.VMEM(part, bf),
             pltpu.VMEM((count - 1,) + part, bf),
-            pltpu.VMEM(part, bf),
             pltpu.VMEM((count,) + part, bf),
             pltpu.VMEM((2 * levels, 2, blocks, rank, rank), bf),
             pltpu.VMEM((2, blocks, rank, CHUNK), bf),
@@ -178,10 +174,9 @@
             pltpu.SemaphoreType.DMA((2 * levels, 2)),
             pltpu.SemaphoreType.DMA((count,)),
             pltpu.SemaphoreType.DMA((count, chunks, blocks)),
-            pltpu.SemaphoreType.DMA,
         ],
         compiler_params=pltpu.CompilerParams(
-            collective_id=0, has_side_effects=True, vmem_limit_bytes=60 * 2**20),
+            collective_id=0, has_side_effects=True, vmem_limit_bytes=56 * 2**20),
     )(
         source.reshape(blocks, rank, rhs),
         row_factors.reshape(levels, blocks, rank, 2 * rank),

time: 123 us -> 121 us (0.984)
  local copies, waits for them, and re-layouts: 3.08 us -> 1.32 us
    unnamed x1, local copies, waits for them, and re-layouts: 3.08 us -> 1.32 us
where the time goes in v2:
time: 121 us; the launch traced here: 120 us
  Pallas kernels  119 us (98%)
  local copies, waits for them, and re-layouts  1.32 us (1%)
    pallas_call x1, Pallas kernels, per_device(): pl.pallas_call(functools.partial(kernel, groups, levels), out_shape=pltpu...  119 us

profile of v2, /device:TPU:4, one launch (start us, length us, event | category | flops | bytes accessed | tf_op | source)
XLA Modules:
  0.0 120.5 jit_solution(10585755758039654901)
XLA Ops:
  0.0 119.1 %shard_map.37 = bf16[4,256,1024]{2,1,0:T(8,128)(2,1)S(1)} custom-call(bf16[4,256,1024]{2,1,0:T(8,128)(2,1)} %bitcast.9, bf16[4,4,256,512]{3,2,1,0:T(8,128)(2,1)} %bitcast.7, bf16[4,4,256,512]{3,2,1,0:T(8,128)(2,1)} %bitcast.8), custom_call_target="tpu_custom_call" | custom-call | tf_op jit(solution)/shard_map/pallas_call | solution.py:162
  119.1 1.3 %copy.6 = bf16[4,1,1,256,1024]{4,3,2,1,0:T(8,128)(2,1)} copy(bf16[4,1,1,256,1024]{4,3,2,1,0:T(8,128)(2,1)S(1)} %bitcast.6) | data formatting | bytes 4194304
